TPU v7x, 32 devices: a whole 2x2x4 slice. The times are simulated.
32 devices in a mesh: row: 4 (over y, core), col: 8 (over z, x).
Axes of the slice: x: 2, y: 2, z: 4, core: 2. Of those that a mesh axis runs over, the one named last changes fastest.
Arguments:
- values: bfloat16 [8192, 128], P('row'), may hold values from -30 to 30
- points0: bfloat16 [2, 8192], P(None, 'row'), may hold values from 0 to 1
- points1: bfloat16 [2, 2048], P(None, 'row'), may hold values from 0 to 1
- points2: bfloat16 [2, 256], P(None, 'row'), may hold values from 0 to 1
- tiles_a0: int32 [4, 8, 2, 48], P('row', 'col'), may hold values from 0 to 15, as said below
- tiles_e1: int32 [4, 8, 2, 20], P('row', 'col'), may hold values from 0 to 15, as said below
- tiles_a1: int32 [4, 8, 2, 4], P('row', 'col'), may hold values from 0 to 3, as said below
- factor: bfloat16 [256, 256], P('row', 'col'), as said below
Outputs:
- fine_coef: float32 [8192, 128], P(('row', 'col'))
- mid_coef: float32 [2048, 128], P('col')
- coarse_coef: float32 [256, 128], P('row')
- norms: float32 [1], replicated
Inputs may be any that keep to these rules, and one draw needn't show every extreme that they name: `tiles_a0`: within each block the 48 listed tile pairs are distinct; tile rows are below 16 and tile columns below 8. `tiles_e1`: within each block the 20 listed tile pairs are distinct; tile rows are below 16 and tile columns below 2. `tiles_a1`: within each block the 4 listed tile pairs are distinct; tile rows are below 4 and tile columns below 2. `factor`: upper triangular; diagonal entries from 1 to 2.
All inputs are finite; a program needn't handle non-finite values.
Results may differ from a plain program's by a relative error of at most 0.0042.
Values may be sent and summed in bfloat16 or wider, within the bound.
A program may use at most 64 MiB of HBM per device.

v0:
```python
import math
import jax
import jax.numpy as jnp
from jax import lax
from jax.sharding import PartitionSpec as P

TILE = 128
support_fine = 0.35
support_mid = 0.55
support_coarse = 0.8


def spread(x, axis, root):
    mine = lax.axis_index(axis) == root
    return lax.psum(jnp.where(mine, x, jnp.zeros_like(x)), axis)


def wendland(left_pts, right_pts, support):
    left = left_pts.astype(jnp.float32)
    right = right_pts.astype(jnp.float32)
    across = left[0][..., :, None] - right[0][..., None, :]
    upward = left[1][..., :, None] - right[1][..., None, :]
    ratio_t = jnp.sqrt(across * across + upward * upward) / support
    margin = jnp.maximum(1.0 - ratio_t, 0.0)
    squared = margin * margin
    return (squared * squared * (4.0 * ratio_t + 1.0)).astype(jnp.bfloat16)


def listed_terms(row_pts, col_pts, listing, vector, support, flipped):
    row_tiles = row_pts.reshape(2, -1, TILE)
    col_tiles = col_pts.reshape(2, -1, TILE)
    listed = listing.shape[-1]
    group = math.gcd(listed, 32)
    order = listing.reshape(2, listed // group, group)
    fields = vector.shape[-1]
    inputs = vector.reshape(-1, TILE, fields)
    target = col_tiles.shape[1] if flipped else row_tiles.shape[1]
    total = jnp.zeros((target, TILE, fields), jnp.float32)

    def add_group(total, pair):
        tile_rows, tile_cols = pair
        kernel = wendland(row_tiles[:, tile_rows], col_tiles[:, tile_cols], support)
        if flipped:
            contrib = jnp.einsum(
                "gij,gir->gjr", kernel, inputs[tile_rows], preferred_element_type=jnp.float32
            )
            return (total.at[tile_cols].add(contrib), None)
        contrib = jnp.einsum(
            "gij,gjr->gir", kernel, inputs[tile_cols], preferred_element_type=jnp.float32
        )
        return (total.at[tile_rows].add(contrib), None)

    total, unused = lax.scan(add_group, total, (order[0], order[1]))
    return total.reshape(-1, fields)


def per_device(values, points0, points1, points2, tiles_a0, tiles_e1, tiles_a1, factor):
    row_count = lax.axis_size("row")
    col_count = lax.axis_size("col")
    col_id = lax.axis_index("col")
    col_per_row = col_count // row_count
    rows_fine, fields = values.shape
    rows_mid = points1.shape[1]
    share = rows_fine // col_count
    cols_fine = rows_fine // col_per_row
    cols_mid = rows_mid // col_per_row
    source = col_id // col_per_row
    part_index = col_id % col_per_row
    value_piece = lax.dynamic_slice_in_dim(values, part_index * cols_fine, cols_fine, 0)
    fine_piece = lax.dynamic_slice_in_dim(points0, part_index * cols_fine, cols_fine, 1)
    mid_piece = lax.dynamic_slice_in_dim(points1, part_index * cols_mid, cols_mid, 1)
    value_cols, fine_cols, mid_cols = (
        spread(value_piece, "row", source),
        spread(fine_piece, "row", source),
        spread(mid_piece, "row", source),
    )
    scale_a0 = (rows_fine / (col_count * tiles_a0.shape[-1] * TILE * TILE)) ** 0.5
    scale_e1 = (rows_fine / (col_count * tiles_e1.shape[-1] * TILE * TILE)) ** 0.5
    scale_a1 = (rows_mid / (col_count * tiles_a1.shape[-1] * TILE * TILE)) ** 0.5
    scale_e2 = (1.0 / (rows_mid * row_count)) ** 0.5
    fine_data = values.astype(jnp.float32)
    own_data = lax.dynamic_slice_in_dim(values, col_id * share, share, 0).astype(jnp.float32)
    product_part = listed_terms(points0, fine_cols, tiles_a0[0, 0], value_cols, support_fine, False)
    product_whole = lax.psum(product_part, "col")
    fine_residual = fine_data - 0.5 * (scale_a0 * product_whole)
    fine_square = jnp.sum(fine_residual * fine_residual)
    restrict_part = listed_terms(
        points0, mid_cols, tiles_e1[0, 0], fine_residual.astype(jnp.bfloat16), support_mid, True
    )
    restrict_sum = lax.psum(restrict_part, "row")
    mid_data = scale_e1 * restrict_sum
    mid_part = listed_terms(
        points1, mid_cols, tiles_a1[0, 0], mid_data.astype(jnp.bfloat16), support_mid, False
    )
    mid_whole = (scale_a1 * lax.psum(mid_part, "col")).astype(jnp.bfloat16)
    mid_slice = lax.dynamic_slice_in_dim(mid_whole, part_index * cols_mid, cols_mid, 0)
    mid_turned = spread(mid_slice, "row", source)
    mid_residual = mid_data - 0.5 * mid_turned.astype(jnp.float32)
    coarse_kernel = wendland(points2, mid_cols, support_coarse)
    coarse_part = jnp.dot(
        coarse_kernel, mid_residual.astype(jnp.bfloat16), preferred_element_type=jnp.float32
    )
    coarse_sum = lax.psum(coarse_part, "col")
    coarse_data = (scale_e2 * coarse_sum).astype(jnp.bfloat16)
    halfway_part = lax.dot_general(
        factor, coarse_data, (((0,), (0,)), ((), ())), preferred_element_type=jnp.float32
    )
    halfway = lax.psum(halfway_part, "row").astype(jnp.bfloat16)
    coarse_part_two = jnp.dot(factor, halfway, preferred_element_type=jnp.float32)
    coarse_coef = lax.psum(coarse_part_two, "col")
    prolong_part = lax.dot_general(
        coarse_kernel,
        coarse_coef.astype(jnp.bfloat16),
        (((0,), (0,)), ((), ())),
        preferred_element_type=jnp.float32,
    )
    mid_coef = 0.5 * mid_data + scale_e2 * lax.psum(prolong_part, "row")
    fine_part = listed_terms(
        points0, mid_cols, tiles_e1[0, 0], mid_coef.astype(jnp.bfloat16), support_mid, False
    )
    fine_coef = 0.5 * own_data + scale_e1 * lax.psum_scatter(
        fine_part, "col", scatter_dimension=0, tiled=True
    )
    fine_total = lax.psum(fine_square / col_count, ("row", "col"))
    fine_norm = fine_total / (rows_fine * row_count * fields)
    return (fine_coef, mid_coef, coarse_coef, jnp.stack([fine_norm]))


def solution(mesh):
    return jax.shard_map(
        per_device,
        mesh=mesh,
        in_specs=(
            P("row", None),
            P(None, "row"),
            P(None, "row"),
            P(None, "row"),
            P("row", "col", None, None),
            P("row", "col", None, None),
            P("row", "col", None, None),
            P("row", "col"),
        ),
        out_specs=(P(("row", "col"), None), P("col", None), P("row", None), P()),
        check_vma=False,
    )
```

profile of v0, /device:TPU:0, one launch (start us, length us, event | category | flops | bytes accessed | tf_op | source)
XLA Modules:
  0.0 501.4 jit_solution(3732552858694689181)
XLA Ops:
  7.3 1.7 dynamic-slice_select_fusion
  11.9 8.5 %all-reduce = (bf16[2,256]{1,0:T(2,128)(2,1)S(1)}, bf16[2,8,128]{2,0,1:T(2,128)(2,1)S(1)}) all-reduce(bf16[2,256]{1,0:T(2,128)(2,1)S(1)} %broadcast_select_fusion.1, bf16[2,8,128]{2,0,1:T(2,128)(2,1)S(1)} %fusion.64), channel_id=1, replica_groups=mesh['row'=4,'col'=8] {'row'}, use_global_device_ids=true, to_apply=%region_0.1 | all-reduce | flops 2560 | bytes 10240 | tf_op jit(solution)/shard_map/psum | solution.py:15
  20.4 24.9 %all-reduce.8.cloned.1.call-done = bf16[8,128,128]{2,1,0:T(8,128)(2,1)} async-done(((bf16[8,128,128]{2,1,0:T(8,128)(2,1)}), bf16[8,128,128]{2,1,0:T(8,128)(2,1)}) %all-reduce.8.cloned.1.call-update) | async-done | bytes 262160 | tf_op jit(solution)/shard_map/psum | solution.py:15
  46.3 15.2 %while.40 = (s32[]{:T(128)}, f32[16,128,128]{2,1,0:T(8,128)S(1)}, s32[3,16]{1,0:T(4,128)S(1)}, bf16[2,16,128]{2,0,1:T(2,128)(2,1)S(1)}, s32[3,16]{1,0:T(4,128)S(...) while((s32[]{:T(128)}, f32[16,128,128]{2,1,0:T(8,128)S(1)}, ...), condition=%wide.region_5.6_spmd, body=%wide.region_3.5_spmd.sunk | while | flops 71051360 | bytes 5956313 | solution.py:53
  48.2 1.5 fusion.118
  49.7 1.6 scatter_fusion
  54.8 1.6 scatter_fusion
  59.9 1.6 scatter_fusion
  63.9 77.0 %all-reduce.10.cloned.1.call-done = f32[2048,128]{1,0:T(8,128)} async-done(((f32[2048,128]{1,0:T(8,128)}), f32[2048,128]{1,0:T(8,128)}) %all-reduce.10.cloned.1.call-update) | async-done | bytes 1048592 | tf_op jit(solution)/shard_map/psum | solution.py:84
  140.9 2.2 multiply_reduce_fusion
  143.1 14.7 %while.41 = (s32[]{:T(128)}, f32[2,128,128]{2,1,0:T(8,128)S(1)}, s32[5,4]{1,0:T(8,128)S(1)}, s32[5,4]{1,0:T(8,128)S(1)}, bf16[2,16,128]{2,0,1:T(2,128)(2,1)S(1)}...) while((s32[]{:T(128)}, f32[2,128,128]{2,1,0:T(8,128)S(1)}, ...), condition=%wide.region_9.10_spmd, body=%wide.region_7.9_spmd.sunk | while | flops 17764376 | bytes 1495289 | solution.py:53
  158.6 31.5 %all-reduce.12.cloned.1.call-done = f32[256,128]{1,0:T(8,128)} async-done(((f32[256,128]{1,0:T(8,128)}), f32[256,128]{1,0:T(8,128)}) %all-reduce.12.cloned.1.call-update) | async-done | bytes 131088 | tf_op jit(solution)/shard_map/psum | solution.py:90
  193.5 71.1 %all-reduce.14.cloned.1.call-done = f32[512,128]{1,0:T(8,128)} async-done(((f32[512,128]{1,0:T(8,128)}), f32[512,128]{1,0:T(8,128)}) %all-reduce.14.cloned.1.call-update) | async-done | bytes 262160 | tf_op jit(solution)/shard_map/psum | solution.py:95
  264.6 1.6 fusion.57
  266.2 31.9 %all-reduce.16.cloned.1.call-done = bf16[256,128]{1,0:T(8,128)(2,1)} async-done(((bf16[256,128]{1,0:T(8,128)(2,1)}), bf16[256,128]{1,0:T(8,128)(2,1)}) %all-reduce.16.cloned.1.call-update) | async-done | bytes 65552 | tf_op jit(solution)/shard_map/psum | solution.py:15
  299.2 37.1 %psum.91 = f32[64,128]{1,0:T(8,128)S(1)} all-reduce(f32[64,128]{1,0:T(8,128)S(1)} %fusion.56), channel_id=1, replica_groups=mesh['row'=4,'col'=8] {'col'}, use_global_device_ids=true, to_apply=%region_14.15 | all-reduce | flops 8192 | bytes 65536 | tf_op jit(solution)/shard_map/psum | solution.py:103
  336.5 10.8 %psum.92 = bf16[32,128]{0,1:T(8,128)(2,1)S(1)} all-reduce(f32[32,128]{0,1:T(8,128)S(1)} %convolution_bitcast_fusion), channel_id=1, replica_groups=mesh['row'=4,'col'=8] {'row'}, use_global_device_ids=true, to_apply=%region_15.16 | all-reduce | flops 4096 | bytes 24576 | tf_op jit(solution)/shard_map/psum | solution.py:108
  347.5 33.0 %psum.93 = f32[64,128]{1,0:T(8,128)S(1)} all-reduce(f32[64,128]{1,0:T(8,128)S(1)} %convolution_bitcast_fusion.1), channel_id=1, replica_groups=mesh['row'=4,'col'=8] {'col'}, use_global_device_ids=true, to_apply=%region_16.17 | all-reduce | flops 8192 | bytes 65536 | tf_op jit(solution)/shard_map/psum | solution.py:110
  381.6 28.0 %all-reduce.18.cloned.1.call-done = f32[256,128]{1,0:T(8,128)} async-done(((f32[256,128]{1,0:T(8,128)}), f32[256,128]{1,0:T(8,128)}) %all-reduce.18.cloned.1.call-update) | async-done | bytes 131088 | tf_op jit(solution)/shard_map/psum | solution.py:117
  409.5 1.6 fusion.82
  411.2 14.8 %while.42 = (s32[]{:T(128)}, f32[16,128,128]{2,1,0:T(8,128)S(1)}, s32[5,4]{1,0:T(8,128)S(1)}, bf16[2,16,128]{2,0,1:T(2,128)(2,1)S(1)}, s32[5,4]{1,0:T(8,128)S(1)...) while((s32[]{:T(128)}, f32[16,128,128]{2,1,0:T(8,128)S(1)}, ...), condition=%wide.region_20.21_spmd, body=%wide.region_18.20_spmd.sunk | while | flops 17764376 | bytes 1495289 | solution.py:53
  427.7 39.5 %psum.95 = f32[]{:T(128)} all-reduce(f32[]{:T(128)S(6)} %div.39), channel_id=1, replica_groups=mesh['row'=4,'col'=8] {'row','col'}, use_global_device_ids=true, to_apply=%region_23.24 | all-reduce | flops 1 | bytes 8 | tf_op jit(solution)/shard_map/psum | solution.py:124
  467.8 24.0 %reduce-scatter.2.cloned.1.call-done = f32[256,128]{1,0:T(8,128)} async-done(((f32[2048,128]{1,0:T(8,128)}), f32[256,128]{1,0:T(8,128)}) %reduce-scatter.2.cloned.1.call-update) | async-done | bytes 131088 | tf_op jit(solution)/shard_map/reduce_scatter | solution.py:121
  491.8 1.6 multiply_add_fusion
  (228 shorter events, 51.4 us)
Async XLA Ops:
  7.2 329.1 %copy-start = (bf16[64,32]{0,1:T(8,128)(2,1)S(1)}, bf16[64,32]{0,1:T(8,128)(2,1)}, u32[]{:S(2)}) copy-start(bf16[64,32]{0,1:T(8,128)(2,1)} %param.21) | copy-start | bytes 12292
  7.2 38.2 %all-reduce.8.cloned.1.call-start = ((), (), s32[]{:S(2)}) async-start(), calls=%async_computation.1 | async-start | bytes 524288 | tf_op jit(solution)/shard_map/psum | solution.py:15
  9.0 131.9 %all-reduce.10.cloned.1.call-start = ((), (), s32[]{:S(2)}) async-start(), calls=%async_computation.2 | async-start | bytes 2097152 | tf_op jit(solution)/shard_map/psum | solution.py:84
  9.0 0.7 copy-start.11
  9.7 0.7 copy-start.12
  10.4 0.7 copy-start.10
  11.2 0.7 copy-start.8
  45.4 0.9 copy-start.2
  61.5 1.0 copy-start.1
  61.5 1.1 copy-start.13
  61.6 79.4 %copy-start.6 = (bf16[2048,128]{1,0:T(8,128)(2,1)S(1)}, bf16[2048,128]{1,0:T(8,128)(2,1)}, u32[]{:S(2)}) copy-start(bf16[2048,128]{1,0:T(8,128)(2,1)} %param.14) | copy-start | bytes 1572868
  62.6 127.5 %all-reduce.12.cloned.1.call-start = ((), (), s32[]{:S(2)}) async-start(), calls=%async_computation.3 | async-start | bytes 262144 | tf_op jit(solution)/shard_map/psum | solution.py:90
  157.9 0.7 copy-start.3
  158.5 106.1 %all-reduce.14.cloned.1.call-start = ((), (), s32[]{:S(2)}) async-start(), calls=%async_computation.4 | async-start | bytes 524288 | tf_op jit(solution)/shard_map/psum | solution.py:95
  192.7 0.7 copy-start.5
  192.7 0.8 copy-start.14
  193.4 104.7 %all-reduce.16.cloned.1.call-start = ((), (), s32[]{:S(2)}) async-start(), calls=%async_computation.5 | async-start | bytes 131072 | tf_op jit(solution)/shard_map/psum | solution.py:15
  193.5 104.6 %copy-start.7 = (f32[256,128]{1,0:T(8,128)S(1)}, f32[256,128]{1,0:T(8,128)}, u32[]{:S(2)}) copy-start(f32[256,128]{1,0:T(8,128)} %all-reduce.12.cloned.1.call-done) | copy-start | bytes 393220
  266.2 143.4 %all-reduce.18.cloned.1.call-start = ((), (), s32[]{:S(2)}) async-start(), calls=%async_computation.6 | async-start | bytes 262144 | tf_op jit(solution)/shard_map/psum | solution.py:117
  380.5 1.0 copy-start.9
  381.5 110.3 %reduce-scatter.2.cloned.1.call-start = ((), (), s32[]{:S(2)}) async-start(), calls=%async_computation.7 | async-start | bytes 1179648 | tf_op jit(solution)/shard_map/reduce_scatter | solution.py:121
  426.0 1.0 copy-start.4
Sparse Core Ops, SparseCore 0:
  10.3 34.9 all-reduce.7
  62.7 78.1 all-reduce.9
  158.7 31.3 all-reduce.11
  193.6 70.9 all-reduce.13
  267.3 30.7 all-reduce.15
  381.6 27.8 all-reduce.17
  427.2 64.5 reduce-scatter.1
where the time goes:
time: 502 us; the launch traced here: 501 us
  waiting for transfers between devices  288 us (57%)
  blocking collectives  129 us (26%)
  local copies, waits for them, and re-layouts  31.9 us (6%)
  other arithmetic  23.1 us (5%)
  between operations  16.8 us (3%)
  matrix products  10.9 us (2%)
    psum x1, waiting for transfers between devices, per_device(): product_whole = lax.psum(product_part, 'col')  77 us
    psum x1, waiting for transfers between devices, per_device(): mid_whole = (scale_a1 * lax.psum(mid_part, 'col')).astype(jnp.bfloat16)  71.1 us
    psum x2, waiting for transfers between devices, spread(): return lax.psum(jnp.where(mine, x, jnp.zeros_like(x)), axis)  56.8 us
    psum x1, blocking collectives, per_device(): fine_total = lax.psum(fine_square / col_count, ('row', 'col'))  39.5 us
    psum x1, blocking collectives, per_device(): coarse_sum = lax.psum(coarse_part, 'col')  37.1 us
    psum x1, blocking collectives, per_device(): coarse_coef = lax.psum(coarse_part_two, 'col')  33 us
    psum x1, waiting for transfers between devices, per_device(): restrict_sum = lax.psum(restrict_part, 'row')  31.5 us
    psum x1, waiting for transfers between devices, per_device(): mid_coef = 0.5 * mid_data + scale_e2 * lax.psum(prolong_part, 'row')  28 us
  transfers between devices with their start and end apart: 7, of which 7 were waited for; matrix products, arithmetic and copies ran while one was open for 0% of the time, Pallas kernels for 0%

commit v1 on v0

--- a/solution.py
+++ b/solution.py
@@ -87,7 +87,8 @@
     restrict_part = listed_terms(
         points0, mid_cols, tiles_e1[0, 0], fine_residual.astype(jnp.bfloat16), support_mid, True
     )
-    restrict_sum = lax.psum(restrict_part, "row")
+    current_value = lax.all_gather(restrict_part, axis_name="row")
+    restrict_sum = jnp.sum(current_value, 0)
     mid_data = scale_e1 * restrict_sum
     mid_part = listed_terms(
         points1, mid_cols, tiles_a1[0, 0], mid_data.astype(jnp.bfloat16), support_mid, False

time: 502 us -> 474 us (0.944)
  waiting for transfers between devices: 288 us -> 256 us
  blocking collectives: 129 us -> 136 us
    psum x1 -> x0, waiting for transfers between devices: 31.5 us -> none  [per_device(): restrict_sum = lax.psum(restrict_part, 'row')]
    all_gather x0 -> x1, blocking collectives: none -> 7.15 us  [per_device(): current_value = lax.all_gather(restrict_part, axis_name='row')]
  transfers between devices with their start and end apart: 7 -> 6, of which waited for: 7 -> 6; matrix products, arithmetic and copies ran while one was open for 0% -> 0% of each run, Pallas kernels for 0% -> 0%
where the time goes in v1:
time: 474 us
  waiting for transfers between devices  256 us (54%)
  blocking collectives  136 us (29%)
  local copies, waits for them, and re-layouts  31.4 us (7%)
  other arithmetic  22.2 us (5%)
  between operations  16.8 us (4%)
  matrix products  10.9 us (2%)
    psum x1, waiting for transfers between devices, per_device(): product_whole = lax.psum(product_part, 'col')  76.9 us
    psum x1, waiting for transfers between devices, per_device(): mid_whole = (scale_a1 * lax.psum(mid_part, 'col')).astype(jnp.bfloat16)  70 us
    psum x2, waiting for transfers between devices, spread(): return lax.psum(jnp.where(mine, x, jnp.zeros_like(x)), axis)  56.6 us
    psum x1, blocking collectives, per_device(): fine_total = lax.psum(fine_square / col_count, ('row', 'col'))  39.6 us
    psum x1, blocking collectives, per_device(): coarse_sum = lax.psum(coarse_part, 'col')  37.1 us
    psum x1, blocking collectives, per_device(): coarse_coef = lax.psum(coarse_part_two, 'col')  33 us
    psum x1, waiting for transfers between devices, per_device(): mid_coef = 0.5 * mid_data + scale_e2 * lax.psum(prolong_part, 'row')  28.1 us
    reduce_scatter x1, waiting for transfers between devices, per_device(): lax.psum_scatter(fine_part, 'col', scatter_dimension=0, tiled=True)  23.9 us
  transfers between devices with their start and end apart: 6, of which 6 were waited for; matrix products, arithmetic and copies ran while one was open for 0% of the time, Pallas kernels for 0%

profile of v1, /device:TPU:0, one launch (start us, length us, event | category | flops | bytes accessed | tf_op | source)
XLA Modules:
  0.0 473.8 jit_solution(5491270841488756216)
XLA Ops:
  7.3 1.7 dynamic-slice_select_fusion
  11.9 8.7 %all-reduce = (bf16[2,256]{1,0:T(2,128)(2,1)S(1)}, bf16[2,8,128]{2,0,1:T(2,128)(2,1)S(1)}) all-reduce(bf16[2,256]{1,0:T(2,128)(2,1)S(1)} %broadcast_select_fusion.1, bf16[2,8,128]{2,0,1:T(2,128)(2,1)S(1)} %fusion.64), channel_id=1, replica_groups=mesh['row'=4,'col'=8] {'row'}, use_global_device_ids=true, to_apply=%region_0.1 | all-reduce | flops 2560 | bytes 10240 | tf_op jit(solution)/shard_map/psum | solution.py:15
  20.7 24.7 %all-reduce.7.cloned.1.call-done = bf16[8,128,128]{2,1,0:T(8,128)(2,1)} async-done(((bf16[8,128,128]{2,1,0:T(8,128)(2,1)}), bf16[8,128,128]{2,1,0:T(8,128)(2,1)}) %all-reduce.7.cloned.1.call-update) | async-done | bytes 262160 | tf_op jit(solution)/shard_map/psum | solution.py:15
  46.3 15.2 %while.40 = (s32[]{:T(128)}, f32[16,128,128]{2,1,0:T(8,128)S(1)}, s32[3,16]{1,0:T(4,128)S(1)}, bf16[2,16,128]{2,0,1:T(2,128)(2,1)S(1)}, s32[3,16]{1,0:T(4,128)S(...) while((s32[]{:T(128)}, f32[16,128,128]{2,1,0:T(8,128)S(1)}, ...), condition=%wide.region_5.6_spmd, body=%wide.region_3.5_spmd.sunk | while | flops 71051360 | bytes 5956313 | solution.py:53
  48.2 1.5 fusion.118
  49.7 1.6 scatter_fusion
  54.8 1.6 scatter_fusion
  59.9 1.6 scatter_fusion
  64.0 76.9 %all-reduce.9.cloned.1.call-done = f32[2048,128]{1,0:T(8,128)} async-done(((f32[2048,128]{1,0:T(8,128)}), f32[2048,128]{1,0:T(8,128)}) %all-reduce.9.cloned.1.call-update) | async-done | bytes 1048592 | tf_op jit(solution)/shard_map/psum | solution.py:84
  140.9 2.2 multiply_reduce_fusion
  143.1 14.8 %while.41 = (s32[]{:T(128)}, f32[2,128,128]{2,1,0:T(8,128)S(1)}, s32[5,4]{1,0:T(8,128)S(1)}, s32[5,4]{1,0:T(8,128)S(1)}, bf16[2,16,128]{2,0,1:T(2,128)(2,1)S(1)}...) while((s32[]{:T(128)}, f32[2,128,128]{2,1,0:T(8,128)S(1)}, ...), condition=%wide.region_9.10_spmd, body=%wide.region_7.9_spmd.sunk | while | flops 17764376 | bytes 1495289 | solution.py:53
  157.9 7.2 %all_gather.3 = f32[4,256,128]{2,1,0:T(8,128)S(1)} all-gather(f32[1,256,128]{2,1,0:T(8,128)S(1)} %bitcast.150), channel_id=1, replica_groups=mesh['row'=4,'col'=8] {'row'}, dimensions={0}, use_global_device_ids=true | all-gather | bytes 655360 | tf_op jit(solution)/shard_map/all_gather | solution.py:90
  167.6 70.0 %all-reduce.11.cloned.1.call-done = f32[512,128]{1,0:T(8,128)} async-done(((f32[512,128]{1,0:T(8,128)}), f32[512,128]{1,0:T(8,128)}) %all-reduce.11.cloned.1.call-update) | async-done | bytes 262160 | tf_op jit(solution)/shard_map/psum | solution.py:96
  237.6 1.6 fusion.57
  239.3 31.9 %all-reduce.13.cloned.1.call-done = bf16[256,128]{1,0:T(8,128)(2,1)} async-done(((bf16[256,128]{1,0:T(8,128)(2,1)}), bf16[256,128]{1,0:T(8,128)(2,1)}) %all-reduce.13.cloned.1.call-update) | async-done | bytes 65552 | tf_op jit(solution)/shard_map/psum | solution.py:15
  272.2 37.1 %psum.83 = f32[64,128]{1,0:T(8,128)S(1)} all-reduce(f32[64,128]{1,0:T(8,128)S(1)} %fusion.56), channel_id=1, replica_groups=mesh['row'=4,'col'=8] {'col'}, use_global_device_ids=true, to_apply=%region_14.15 | all-reduce | flops 8192 | bytes 65536 | tf_op jit(solution)/shard_map/psum | solution.py:104
  309.4 10.2 %psum.84 = bf16[32,128]{1,0:T(8,128)(2,1)S(1)} all-reduce(f32[32,128]{1,0:T(8,128)S(1)} %convolution_bitcast_fusion.1), channel_id=1, replica_groups=mesh['row'=4,'col'=8] {'row'}, use_global_device_ids=true, to_apply=%region_15.16 | all-reduce | flops 4096 | bytes 24576 | tf_op jit(solution)/shard_map/psum | solution.py:109
  319.8 33.0 %psum.85 = f32[64,128]{1,0:T(8,128)S(1)} all-reduce(f32[64,128]{1,0:T(8,128)S(1)} %convolution_bitcast_fusion), channel_id=1, replica_groups=mesh['row'=4,'col'=8] {'col'}, use_global_device_ids=true, to_apply=%region_16.17 | all-reduce | flops 8192 | bytes 65536 | tf_op jit(solution)/shard_map/psum | solution.py:111
  353.9 28.1 %all-reduce.15.cloned.1.call-done = f32[256,128]{1,0:T(8,128)} async-done(((f32[256,128]{1,0:T(8,128)}), f32[256,128]{1,0:T(8,128)}) %all-reduce.15.cloned.1.call-update) | async-done | bytes 131088 | tf_op jit(solution)/shard_map/psum | solution.py:118
  382.0 1.6 fusion.82
  383.6 14.8 %while.42 = (s32[]{:T(128)}, f32[16,128,128]{2,1,0:T(8,128)S(1)}, s32[5,4]{1,0:T(8,128)S(1)}, bf16[2,16,128]{2,0,1:T(2,128)(2,1)S(1)}, s32[5,4]{1,0:T(8,128)S(1)...) while((s32[]{:T(128)}, f32[16,128,128]{2,1,0:T(8,128)S(1)}, ...), condition=%wide.region_20.21_spmd, body=%wide.region_18.20_spmd.sunk | while | flops 17764376 | bytes 1495289 | solution.py:53
  400.1 39.6 %psum.87 = f32[]{:T(128)} all-reduce(f32[]{:T(128)S(6)} %div.39), channel_id=1, replica_groups=mesh['row'=4,'col'=8] {'row','col'}, use_global_device_ids=true, to_apply=%region_23.24 | all-reduce | flops 1 | bytes 8 | tf_op jit(solution)/shard_map/psum | solution.py:125
  440.3 23.9 %reduce-scatter.2.cloned.1.call-done = f32[256,128]{1,0:T(8,128)} async-done(((f32[2048,128]{1,0:T(8,128)}), f32[256,128]{1,0:T(8,128)}) %reduce-scatter.2.cloned.1.call-update) | async-done | bytes 131088 | tf_op jit(solution)/shard_map/reduce_scatter | solution.py:122
  464.2 1.6 multiply_add_fusion
  (223 shorter events, 50.0 us)
Async XLA Ops:
  7.2 302.1 %copy-start = (bf16[64,32]{0,1:T(8,128)(2,1)S(1)}, bf16[64,32]{0,1:T(8,128)(2,1)}, u32[]{:S(2)}) copy-start(bf16[64,32]{0,1:T(8,128)(2,1)} %param.21) | copy-start | bytes 12292
  7.2 38.2 %all-reduce.7.cloned.1.call-start = ((), (), s32[]{:S(2)}) async-start(), calls=%async_computation.1 | async-start | bytes 524288 | tf_op jit(solution)/shard_map/psum | solution.py:15
  9.0 0.7 copy-start.6
  9.0 131.9 %all-reduce.9.cloned.1.call-start = ((), (), s32[]{:S(2)}) async-start(), calls=%async_computation.2 | async-start | bytes 2097152 | tf_op jit(solution)/shard_map/psum | solution.py:84
  9.7 0.7 copy-start.9
  10.4 0.7 copy-start.10
  11.0 0.7 copy-start.8
  11.9 8.7 %copy-start.11 = (s32[1,1,2,20]{3,2,1,0:T(2,128)S(1)}, s32[1,1,2,20]{3,2,1,0:T(2,128)}, u32[]{:S(2)}) copy-start(s32[1,1,2,20]{3,2,1,0:T(2,128)} %param.19) | copy-start | bytes 484
  45.4 0.9 copy-start.2
  61.5 1.0 copy-start.1
  61.5 79.4 %copy-start.5 = (bf16[2048,128]{1,0:T(8,128)(2,1)S(1)}, bf16[2048,128]{1,0:T(8,128)(2,1)}, u32[]{:S(2)}) copy-start(bf16[2048,128]{1,0:T(8,128)(2,1)} %param.14) | copy-start | bytes 1572868
  62.6 175.0 %all-reduce.11.cloned.1.call-start = ((), (), s32[]{:S(2)}) async-start(), calls=%async_computation.3 | async-start | bytes 524288 | tf_op jit(solution)/shard_map/psum | solution.py:96
  166.8 0.7 copy-start.4
  166.8 0.8 copy-start.12
  167.5 103.6 %all-reduce.13.cloned.1.call-start = ((), (), s32[]{:S(2)}) async-start(), calls=%async_computation.4 | async-start | bytes 131072 | tf_op jit(solution)/shard_map/psum | solution.py:15
  239.2 142.8 %all-reduce.15.cloned.1.call-start = ((), (), s32[]{:S(2)}) async-start(), calls=%async_computation.5 | async-start | bytes 262144 | tf_op jit(solution)/shard_map/psum | solution.py:118
  352.8 1.0 copy-start.7
  353.8 110.4 %reduce-scatter.2.cloned.1.call-start = ((), (), s32[]{:S(2)}) async-start(), calls=%async_computation.6 | async-start | bytes 1179648 | tf_op jit(solution)/shard_map/reduce_scatter | solution.py:122
  398.4 1.0 copy-start.3
Sparse Core Ops, SparseCore 0:
  10.3 34.9 all-reduce.6
  62.7 78.1 all-reduce.8
  167.6 69.9 all-reduce.10
  240.4 30.7 all-reduce.12
  353.9 27.9 all-reduce.14
  399.6 64.5 reduce-scatter.1
